TPU v7x, 32 devices: a whole 2x2x4 slice. The times are simulated.
32 devices in a mesh: dp: 8 (over z, y), mp: 4 (over x, core).
Axes of the slice: x: 2, y: 2, z: 4, core: 2. Of those that a mesh axis runs over, the one named last changes fastest.
Arguments:
- tokens: bfloat16 [6144, 768], P(('dp', 'mp')), may hold values from -6 to 6
- obs_mask: int32 [96, 64], P(('dp', 'mp')), may hold values 0 or 1
- norm_gains: float32 [5, 768], replicated, may hold values from 0.1 to 1.9
- attn_in: bfloat16 [2, 3, 768, 768], P(None, None, 'dp', 'mp'), may hold values from -0.21875 to 0.21875
- attn_out: bfloat16 [2, 768, 768], P(None, 'mp', 'dp'), may hold values from -0.21875 to 0.21875
- mlp_in: bfloat16 [2, 768, 3072], P(None, 'dp', 'mp'), may hold values from -0.21875 to 0.21875
- mlp_out: bfloat16 [2, 3072, 768], P(None, 'mp', 'dp'), may hold values from -0.109375 to 0.109375
- embodiment: int32 [96, 1], P('dp'), may hold values from 0 to 24; in each aligned block of 12 rows (0 to 11, 12 to 23, ...) no two rows name the same one
- levels: int32 [96, 2], P('dp'), may hold values from 0 to 19
- actions: bfloat16 [96, 2, 56], P('dp'), may hold values from -1 to 1
- noise: bfloat16 [96, 2, 56], P('dp'), may hold values from -5 to 5
- action_dims: int32 [25], replicated, may hold values from 7 to 14
- head_read: bfloat16 [32, 768, 256], P('dp'), may hold values from -0.21875 to 0.21875
- head_act: bfloat16 [32, 56, 256], P('dp'), may hold values from -0.75 to 0.75
- time_table: bfloat16 [32, 20, 256], P('dp'), may hold values from -5 to 5
- block_in: bfloat16 [32, 256, 256], P('dp'), may hold values from -0.375 to 0.375
- block_out: bfloat16 [32, 256, 256], P('dp'), may hold values from -0.375 to 0.375
- head_out: bfloat16 [32, 256, 56], P('dp'), may hold values from -0.375 to 0.375
Outputs:
- readout_grad: bfloat16 [96, 2, 768], P(('dp', 'mp'))
- grad_read: float32 [32, 768, 256], P('dp', 'mp')
- grad_act: float32 [32, 56, 256], P('dp')
- grad_time: float32 [32, 20, 256], P('dp')
- grad_block_in: float32 [32, 256, 256], P('dp')
- grad_block_out: float32 [32, 256, 256], P('dp')
- grad_head_out: float32 [32, 256, 56], P('dp')
Inputs may be any that keep to these rules, and one draw needn't show every extreme that they name: Within each aligned block of 12 samples (those of one dp index) no embodiment appears twice; every embodiment appears in some block.
All inputs are finite; a program needn't handle non-finite values. No bound on the sum of `obs_mask` on one device may be relied on, other than what follows from the above.
Results may differ from a plain program's by a relative error of at most 0.024.
Values may be sent and summed in bfloat16 or wider, within the bound.
A program may use at most 64 MiB of HBM per device.

v0:
```python
import math
import jax
import jax.numpy as jnp
from jax import lax
from jax.sharding import PartitionSpec as P

D = 768
HDIM = 64
EMB = 25
READ = 2
LEVELS = 20
ADIM_MAX = 14
ACT = 56
norm_eps = 1e-05


def normalize(values, scale_gain):
    center = values - jnp.mean(values, axis=-1, keepdims=True)
    spread = jnp.mean(center * center, axis=-1, keepdims=True)
    return center * lax.rsqrt(spread + norm_eps) * scale_gain


def allowed_keys(observed):
    length = observed.shape[1]
    position = jnp.arange(length)
    visible = (observed == 1) & (position < length - READ)[None, :]
    itself = position[:, None] == position[None, :]
    return visible[:, None, :] | itself[None, :, :]


def attend(queries, key_rows, value_rows, allowed):
    scores = jnp.einsum(
        "sqhd,skhd->shqk", queries, key_rows, preferred_element_type=jnp.float32
    ) * HDIM ** (-0.5)
    weights = jnp.where(allowed[:, None, :, :], jnp.exp(scores), 0.0)
    shares = (weights / jnp.sum(weights, axis=-1, keepdims=True)).astype(jnp.bfloat16)
    context = jnp.einsum("shqk,skhd->sqhd", shares, value_rows, preferred_element_type=jnp.float32)
    return context.astype(jnp.bfloat16)


def plan():
    steps_up = (jnp.arange(LEVELS, dtype=jnp.float32) + 1.0) / LEVELS
    anchor = math.cos(0.008 / 1.008 * math.pi / 2) ** 2
    return jnp.cos((steps_up + 0.008) / 1.008 * (math.pi / 2)) ** 2 / anchor


def noisy_pair(level_ids, clean, noise_draw, table):
    picked = (level_ids[..., None] == jnp.arange(LEVELS)).astype(jnp.float32)
    kept = jnp.sum(picked * table, axis=-1)[..., None]
    mixed = jnp.sqrt(kept) * clean.astype(jnp.float32) + jnp.sqrt(1.0 - kept) * noise_draw.astype(
        jnp.float32
    )
    return mixed.astype(jnp.bfloat16)


def tail(first, target, weight_mask, inner_weight, outer_weight, final_weight):
    highest = lax.Precision.HIGHEST
    active = jax.nn.silu(first).astype(jnp.bfloat16)
    inner = jnp.dot(active, inner_weight, preferred_element_type=jnp.float32, precision=highest)
    second = jax.nn.silu(inner).astype(jnp.bfloat16)
    hidden = first + jnp.dot(
        second, outer_weight, preferred_element_type=jnp.float32, precision=highest
    )
    third = jax.nn.silu(hidden).astype(jnp.bfloat16)
    predicted = jnp.dot(third, final_weight, preferred_element_type=jnp.float32, precision=highest)
    differ = predicted - target
    return 0.5 * jnp.sum(weight_mask * differ * differ)


def gather_rows(normed, observed):
    return (
        lax.all_gather(normed, "mp", axis=0, tiled=True),
        lax.all_gather(observed, "mp", axis=0, tiled=True),
    )


def reduce_rows(partial_value):
    return lax.psum_scatter(
        partial_value.astype(jnp.bfloat16), "mp", scatter_dimension=0, tiled=True
    ).astype(jnp.float32)


def head_grads(first, inner_weight, outer_weight, final_weight, target, weight_mask):

    def head_loss(first_in, inner_in, outer_in, final_in):
        return tail(first_in, target, weight_mask, inner_in, outer_in, final_in)

    loss_value, pullback = jax.vjp(head_loss, first, inner_weight, outer_weight, final_weight)
    return pullback(jnp.ones((), jnp.float32))


def on_device(
    tokens,
    obs_mask,
    norm_gains,
    attn_in,
    attn_out,
    mlp_in,
    mlp_out,
    embodiment,
    levels,
    actions,
    noise,
    action_dims,
    head_read,
    head_act,
    time_table,
    block_in,
    block_out,
    head_out,
):
    group_width = attn_in.shape[3]
    heads_local = group_width // HDIM
    samples_local = obs_mask.shape[0]
    length = obs_mask.shape[1]
    layer_count = attn_in.shape[0]
    residual = tokens.astype(jnp.float32)
    for layer_index in range(layer_count):
        normed = normalize(residual, norm_gains[2 * layer_index]).astype(jnp.bfloat16)
        gathered, mask_group = gather_rows(normed, obs_mask)
        samples_group = mask_group.shape[0]
        columns = gathered
        projected = jnp.einsum(
            "td,jdc->jtc",
            columns,
            lax.all_gather(attn_in[layer_index], "dp", axis=1, tiled=True),
            preferred_element_type=jnp.float32,
        )
        projected = projected.astype(jnp.bfloat16).reshape(
            3, samples_group, length, heads_local, HDIM
        )
        context = attend(
            projected[0], projected[1], projected[2], allowed_keys(mask_group)
        ).reshape(-1, group_width)
        partial_value = jnp.dot(
            context,
            lax.all_gather(attn_out[layer_index], "dp", axis=1, tiled=True),
            preferred_element_type=jnp.float32,
        )
        residual = residual + reduce_rows(partial_value)
        normed = normalize(residual, norm_gains[2 * layer_index + 1]).astype(jnp.bfloat16)
        gathered, mask_group = gather_rows(normed, obs_mask)
        raised = jnp.dot(
            gathered,
            lax.all_gather(mlp_in[layer_index], "dp", axis=0, tiled=True),
            preferred_element_type=jnp.float32,
        )
        hidden = jax.nn.gelu(raised, approximate=True).astype(jnp.bfloat16)
        partial_value = jnp.dot(
            hidden,
            lax.all_gather(mlp_out[layer_index], "dp", axis=1, tiled=True),
            preferred_element_type=jnp.float32,
        )
        residual = residual + reduce_rows(partial_value)
    ending = residual.reshape(samples_local, length, D)[:, length - READ :, :]
    readouts = normalize(ending, norm_gains[2 * layer_count]).astype(jnp.bfloat16)
    table = plan()
    heads_dev = head_read.shape[0]
    peers = lax.axis_size("dp")
    slot_count = heads_dev * peers
    my_model = lax.axis_index("mp")
    my_owner = lax.axis_index("dp")
    features = lax.all_to_all(readouts, "mp", split_axis=2, concat_axis=0, tiled=True)
    owners = embodiment[:, 0]
    feature_width = features.shape[2]
    paired = jnp.concatenate([noisy_pair(levels, actions, noise, table), noise], axis=-1)
    send_features = (
        jnp.zeros((slot_count, READ, feature_width), jnp.bfloat16).at[owners].set(features)
    )
    send_paired = jnp.zeros((slot_count, READ, 2 * ACT), jnp.bfloat16).at[owners].set(paired)
    send_levels = jnp.full((slot_count, READ), -1, jnp.int32).at[owners].set(levels)
    got_features, got_paired, got_levels = (
        lax.all_to_all(
            send_features.reshape(peers, heads_dev * READ, feature_width),
            "dp",
            split_axis=0,
            concat_axis=0,
            tiled=True,
        ),
        lax.all_to_all(
            send_paired.reshape(peers, heads_dev * READ, 2 * ACT),
            "dp",
            split_axis=0,
            concat_axis=0,
            tiled=True,
        ),
        lax.all_to_all(
            send_levels.reshape(peers, heads_dev * READ),
            "dp",
            split_axis=0,
            concat_axis=0,
            tiled=True,
        ),
    )

    def by_head(values):
        trailing = values.shape[2:]
        values = values.reshape((peers, heads_dev, READ) + trailing)
        values = jnp.moveaxis(values, 1, 0)
        return values.reshape((heads_dev, peers * READ) + trailing)

    head_features = by_head(got_features)
    head_paired = by_head(got_paired)
    head_levels = by_head(got_levels)
    head_noisy = head_paired[..., :ACT]
    head_target = head_paired[..., ACT:].astype(jnp.float32)
    head_onehot = (head_levels[..., None] == jnp.arange(LEVELS)).astype(jnp.bfloat16)
    slot_ids = my_owner * heads_dev + jnp.arange(heads_dev)
    dims_here = jnp.sum(
        jnp.where(jnp.arange(EMB)[None, :] == slot_ids[:, None], action_dims[None, :], 0), axis=1
    )
    column = jnp.arange(ACT) % ADIM_MAX
    weight_mask = (head_levels >= 0).astype(jnp.float32)[..., None] * (
        column[None, None, :] < dims_here[:, None, None]
    ).astype(jnp.float32)
    others = jnp.einsum("hna,hac->hnc", head_noisy, head_act, preferred_element_type=jnp.float32)
    others = others + jnp.einsum(
        "hnl,hlc->hnc", head_onehot, time_table, preferred_element_type=jnp.float32
    )
    read_weight = lax.dynamic_slice_in_dim(head_read, my_model * feature_width, feature_width, 1)
    first = (
        lax.psum(
            jnp.einsum(
                "hnd,hdc->hnc", head_features, read_weight, preferred_element_type=jnp.float32
            ).astype(jnp.bfloat16),
            "mp",
        ).astype(jnp.float32)
        + others
    )
    grad_first, grad_inner, grad_outer, grad_final = jax.vmap(head_grads)(
        first,
        block_in.astype(jnp.float32),
        block_out.astype(jnp.float32),
        head_out.astype(jnp.float32),
        head_target,
        weight_mask,
    )
    grad_bf = grad_first.astype(jnp.bfloat16)
    grad_readin = jnp.einsum(
        "hnd,hnc->hdc", head_features, grad_bf, preferred_element_type=jnp.float32
    )
    grad_actin = jnp.einsum("hna,hnc->hac", head_noisy, grad_bf, preferred_element_type=jnp.float32)
    grad_timein = jnp.einsum(
        "hnl,hnc->hlc", head_onehot, grad_bf, preferred_element_type=jnp.float32
    )
    backward = jnp.einsum(
        "hnc,hdc->hnd", grad_bf, read_weight, preferred_element_type=jnp.float32
    ).astype(jnp.bfloat16)
    backward = jnp.moveaxis(backward.reshape(heads_dev, peers, READ, feature_width), 0, 1).reshape(
        peers, heads_dev * READ, feature_width
    )
    arrived = lax.all_to_all(backward, "dp", split_axis=0, concat_axis=0, tiled=True)
    arrived = arrived.reshape(slot_count, READ, feature_width)[owners]
    arrived = lax.all_to_all(arrived, "mp", split_axis=0, concat_axis=2, tiled=True)
    return (arrived, grad_readin, grad_actin, grad_timein, grad_inner, grad_outer, grad_final)


def solution(mesh):
    placed = (
        P(("dp", "mp"), None),
        P(("dp", "mp"), None),
        P(),
        P(None, None, "dp", "mp"),
        P(None, "mp", "dp"),
        P(None, "dp", "mp"),
        P(None, "mp", "dp"),
        P("dp", None),
        P("dp", None),
        P("dp", None, None),
        P("dp", None, None),
        P(),
        P("dp", None, None),
        P("dp", None, None),
        P("dp", None, None),
        P("dp", None, None),
        P("dp", None, None),
        P("dp", None, None),
    )
    return jax.shard_map(
        on_device,
        mesh=mesh,
        in_specs=placed,
        out_specs=(
            P(("dp", "mp"), None, None),
            P("dp", "mp", None),
            P("dp", None, None),
            P("dp", None, None),
            P("dp", None, None),
            P("dp", None, None),
            P("dp", None, None),
        ),
        check_vma=False,
    )
```

profile of v0, /device:TPU:0, one launch (start us, length us, event | category | flops | bytes accessed | tf_op | source)
XLA Modules:
  0.0 542.9 jit_solution(12618972121489949078)
XLA Ops:
  14.1 38.8 %all-gather = bf16[1,3,768,192]{3,1,0,2:T(4,128)(2,1)S(1)} all-gather(bf16[1,3,96,192]{3,1,0,2:T(4,128)(2,1)S(1)} %copy.243), channel_id=2, replica_groups=mesh['dp'=8,'mp'=4] {'dp'}, dimensions={2}, use_global_device_ids=true | all-gather | bytes 995328 | tf_op jit(solution)/shard_map/all_gather | solution.py:126
  54.9 5.2 all-gather.8
  61.5 32.1 %all-gather.1 = bf16[1,192,768]{1,0,2:T(2,128)(2,1)S(1)} all-gather(bf16[1,192,96]{1,0,2:T(2,128)(2,1)S(1)} %copy.244), channel_id=3, replica_groups=mesh['dp'=8,'mp'=4] {'dp'}, dimensions={2}, use_global_device_ids=true | all-gather | bytes 331776 | tf_op jit(solution)/shard_map/all_gather | solution.py:137
  110.1 23.1 %reduce-scatter.5.cloned.1.call-done = bf16[192,768]{1,0:T(8,128)(2,1)} async-done(((bf16[768,768]{1,0:T(8,128)(2,1)}), bf16[192,768]{1,0:T(8,128)(2,1)}) %reduce-scatter.5.cloned.1.call-update) | async-done | bytes 294928 | tf_op jit(solution)/shard_map/reduce_scatter | solution.py:78
  136.5 15.6 %all-gather.26.cloned.1.call-done = bf16[1,768,768]{2,1,0:T(8,128)(2,1)} async-done(((bf16[1,96,768]{2,1,0:T(8,128)(2,1)}), bf16[1,768,768]{2,1,0:T(8,128)(2,1)}) %all-gather.26.cloned.1.call-update) | async-done | bytes 1179664 | tf_op jit(solution)/shard_map/all_gather | solution.py:145
  152.1 42.4 %all-gather.28.cloned.1.call-done = bf16[1,768,768]{1,2,0:T(8,128)(2,1)} async-done(((bf16[1,768,96]{1,2,0:T(8,128)(2,1)}), bf16[1,768,768]{1,2,0:T(8,128)(2,1)}) %all-gather.28.cloned.1.call-update) | async-done | bytes 1179664 | tf_op jit(solution)/shard_map/all_gather | solution.py:151
  194.5 17.7 %all-gather.20.cloned.1.call-done = bf16[768,768]{1,0:T(8,128)(2,1)} async-done(((bf16[192,768]{1,0:T(8,128)(2,1)}), bf16[768,768]{1,0:T(8,128)(2,1)}) %all-gather.20.cloned.1.call-update) | async-done | bytes 1179664 | tf_op jit(solution)/shard_map/all_gather | solution.py:72
  212.2 5.2 convolution_convert_fusion.2
  217.5 25.7 %reduce-scatter.7.cloned.1.call-done = bf16[192,768]{1,0:T(8,128)(2,1)} async-done(((bf16[768,768]{1,0:T(8,128)(2,1)}), bf16[192,768]{1,0:T(8,128)(2,1)}) %reduce-scatter.7.cloned.1.call-update) | async-done | bytes 294928 | tf_op jit(solution)/shard_map/reduce_scatter | solution.py:78
  245.7 38.6 %all-gather.4 = bf16[1,3,768,192]{3,1,0,2:T(4,128)(2,1)} all-gather(bf16[1,3,96,192]{3,1,0,2:T(4,128)(2,1)S(1)} %copy.245), channel_id=6, replica_groups=mesh['dp'=8,'mp'=4] {'dp'}, dimensions={2}, use_global_device_ids=true | all-gather | bytes 995328 | tf_op jit(solution)/shard_map/all_gather | solution.py:126
  284.3 3.4 copy.218
  287.8 32.2 %all-gather.5 = bf16[1,192,768]{1,0,2:T(2,128)(2,1)S(1)} all-gather(bf16[1,192,96]{1,0,2:T(2,128)(2,1)S(1)} %copy.246), channel_id=7, replica_groups=mesh['dp'=8,'mp'=4] {'dp'}, dimensions={2}, use_global_device_ids=true | all-gather | bytes 331776 | tf_op jit(solution)/shard_map/all_gather | solution.py:137
  337.1 22.9 %reduce-scatter.9.cloned.1.call-done = bf16[192,768]{1,0:T(8,128)(2,1)} async-done(((bf16[768,768]{1,0:T(8,128)(2,1)}), bf16[192,768]{1,0:T(8,128)(2,1)}) %reduce-scatter.9.cloned.1.call-update) | async-done | bytes 294928 | tf_op jit(solution)/shard_map/reduce_scatter | solution.py:78
  363.3 15.3 %all-gather.30.cloned.1.call-done = bf16[1,768,768]{2,1,0:T(8,128)(2,1)} async-done(((bf16[1,96,768]{2,1,0:T(8,128)(2,1)}), bf16[1,768,768]{2,1,0:T(8,128)(2,1)}) %all-gather.30.cloned.1.call-update) | async-done | bytes 1179664 | tf_op jit(solution)/shard_map/all_gather | solution.py:145
  378.6 42.6 %all-gather.32.cloned.1.call-done = bf16[1,768,768]{1,2,0:T(8,128)(2,1)} async-done(((bf16[1,768,96]{1,2,0:T(8,128)(2,1)}), bf16[1,768,768]{1,2,0:T(8,128)(2,1)}) %all-gather.32.cloned.1.call-update) | async-done | bytes 1179664 | tf_op jit(solution)/shard_map/all_gather | solution.py:151
  421.2 17.7 %all-gather.24.cloned.1.call-done = bf16[768,768]{1,0:T(8,128)(2,1)} async-done(((bf16[192,768]{1,0:T(8,128)(2,1)}), bf16[768,768]{1,0:T(8,128)(2,1)}) %all-gather.24.cloned.1.call-update) | async-done | bytes 1179664 | tf_op jit(solution)/shard_map/all_gather | solution.py:72
  438.8 5.2 convolution_convert_fusion
  446.1 5.5 %all-to-all-start = ((s32[8,1,8]{2,1,0:T(1,128)}), s32[8,1,8]{2,1,0:T(1,128)S(1)}, u32[]{:S(2)}, u32[]{:S(2)}) async-start(s32[8,1,8]{2,1,0:T(1,128)} %bitcast.1), calls=%async_computation | async-start | bytes 8192 | tf_op jit(solution)/shard_map/all_to_all | solution.py:187
  461.6 8.3 %reduce-scatter.11.cloned.1.call-done = bf16[192,768]{1,0:T(8,128)(2,1)} async-done(((bf16[768,768]{1,0:T(8,128)(2,1)}), bf16[192,768]{1,0:T(8,128)(2,1)}) %reduce-scatter.11.cloned.1.call-update) | async-done | bytes 294928 | tf_op jit(solution)/shard_map/reduce_scatter | solution.py:78
  475.8 3.6 all-to-all-start.1
  485.8 5.5 %all-to-all-start.2 = ((bf16[8,8,192]{2,1,0:T(8,128)(2,1)}), bf16[8,8,192]{2,1,0:T(8,128)(2,1)S(1)}, u32[]{:S(2)}, u32[]{:S(2)}) async-start(bf16[8,8,192]{2,1,0:T(8,128)(2,1)} %reshape.234), calls=%async_computation.6 | async-start | bytes 65536 | tf_op jit(solution)/shard_map/all_to_all | solution.py:173
  491.5 6.5 %all-to-all-done.2 = bf16[8,8,192]{2,1,0:T(8,128)(2,1)S(1)} async-done(((bf16[8,8,192]{2,1,0:T(8,128)(2,1)}), bf16[8,8,192]{2,1,0:T(8,128)(2,1)S(1)}, u32[]{:S(2)}, u32[]{:S(2)}) %all-to-all-start.2) | async-done | bytes 24608 | tf_op jit(solution)/shard_map/all_to_all | solution.py:173
  498.3 10.3 %psum.7 = bf16[4,16,256]{2,1,0:T(8,128)(2,1)S(1)} all-reduce(bf16[4,16,256]{2,1,0:T(8,128)(2,1)S(1)} %convolution_convert_fusion.10), channel_id=1, replica_groups=mesh['dp'=8,'mp'=4] {'mp'}, use_global_device_ids=true, to_apply=%region_19.20 | all-reduce | flops 16384 | bytes 65536 | tf_op jit(solution)/shard_map/psum | solution.py:222
  521.1 5.7 %all-to-all-done.4 = bf16[8,8,192]{2,1,0:T(8,128)(2,1)S(1)} async-done(((bf16[8,8,192]{2,1,0:T(8,128)(2,1)}), bf16[8,8,192]{2,1,0:T(8,128)(2,1)S(1)}, u32[]{:S(2)}, u32[]{:S(2)}) %all-to-all-start.4) | async-done | bytes 24608 | tf_op jit(solution)/shard_map/all_to_all | solution.py:252
  (206 shorter events, 97.9 us)
Async XLA Ops:
  8.0 490.1 %copy-start = (bf16[4,768,256]{2,1,0:T(8,128)(2,1)S(1)}, bf16[4,768,256]{2,1,0:T(8,128)(2,1)}, u32[]{:S(2)}) copy-start(bf16[4,768,256]{2,1,0:T(8,128)(2,1)} %param.30) | copy-start | bytes 4718596
  8.0 87.6 %all-gather.18.cloned.1.call-start = ((), (), s32[]{:S(2)}) async-start(), calls=%async_computation.10 | async-start | bytes 1474560 | tf_op jit(solution)/shard_map/all_gather | solution.py:72
  13.3 119.9 %reduce-scatter.5.cloned.1.call-start = ((), (), s32[]{:S(2)}) async-start(), calls=%async_computation.11 | async-start | bytes 1474560 | tf_op jit(solution)/shard_map/reduce_scatter | solution.py:78
  60.7 34.9 %copy-start.6 = (bf16[1,3,768,192]{2,3,1,0:T(8,128)(2,1)S(1)}, bf16[1,3,768,192]{2,3,1,0:T(8,128)(2,1)}, u32[]{:S(2)}) copy-start(bf16[1,3,768,192]{2,3,1,0:T(8,128)(2,1)} %copy.209) | copy-start | bytes 2654212
  108.3 24.9 %copy-start.1 = (bf16[192,768]{1,0:T(8,128)(2,1)S(1)}, bf16[192,768]{1,0:T(8,128)(2,1)}, u32[]{:S(2)}) copy-start(bf16[192,768]{1,0:T(8,128)(2,1)} %param.18) | copy-start | bytes 884740
  108.3 43.8 %all-gather.26.cloned.1.call-start = ((), (), s32[]{:S(2)}) async-start(), calls=%async_computation.18 | async-start | bytes 1327104 | tf_op jit(solution)/shard_map/all_gather | solution.py:145
  109.2 85.4 %all-gather.28.cloned.1.call-start = ((), (), s32[]{:S(2)}) async-start(), calls=%async_computation.19 | async-start | bytes 1327104 | tf_op jit(solution)/shard_map/all_gather | solution.py:151
  110.0 102.2 %all-gather.20.cloned.1.call-start = ((), (), s32[]{:S(2)}) async-start(), calls=%async_computation.12 | async-start | bytes 1474560 | tf_op jit(solution)/shard_map/all_gather | solution.py:72
  136.5 106.7 %reduce-scatter.7.cloned.1.call-start = ((), (), s32[]{:S(2)}) async-start(), calls=%async_computation.13 | async-start | bytes 1474560 | tf_op jit(solution)/shard_map/reduce_scatter | solution.py:78
  217.5 103.1 %all-gather.22.cloned.1.call-start = ((), (), s32[]{:S(2)}) async-start(), calls=%async_computation.14 | async-start | bytes 1474560 | tf_op jit(solution)/shard_map/all_gather | solution.py:72
  245.5 114.5 %reduce-scatter.9.cloned.1.call-start = ((), (), s32[]{:S(2)}) async-start(), calls=%async_computation.15 | async-start | bytes 1474560 | tf_op jit(solution)/shard_map/reduce_scatter | solution.py:78
  335.6 43.0 %all-gather.30.cloned.1.call-start = ((), (), s32[]{:S(2)}) async-start(), calls=%async_computation.20 | async-start | bytes 1327104 | tf_op jit(solution)/shard_map/all_gather | solution.py:145
  336.3 84.9 %all-gather.32.cloned.1.call-start = ((), (), s32[]{:S(2)}) async-start(), calls=%async_computation.21 | async-start | bytes 1327104 | tf_op jit(solution)/shard_map/all_gather | solution.py:151
  337.0 101.8 %all-gather.24.cloned.1.call-start = ((), (), s32[]{:S(2)}) async-start(), calls=%async_computation.16 | async-start | bytes 1474560 | tf_op jit(solution)/shard_map/all_gather | solution.py:72
  363.2 106.6 %reduce-scatter.11.cloned.1.call-start = ((), (), s32[]{:S(2)}) async-start(), calls=%async_computation.17 | async-start | bytes 1474560 | tf_op jit(solution)/shard_map/reduce_scatter | solution.py:78
  446.1 11.9 %all-to-all-start = ((s32[8,1,8]{2,1,0:T(1,128)}), s32[8,1,8]{2,1,0:T(1,128)S(1)}, u32[]{:S(2)}, u32[]{:S(2)}) async-start(s32[8,1,8]{2,1,0:T(1,128)} %bitcast.1), calls=%async_computation | async-start | bytes 8192 | tf_op jit(solution)/shard_map/all_to_all | solution.py:187
  458.0 17.7 %all-to-all-start.3 = ((bf16[8,8,112]{2,1,0:T(8,128)(2,1)}), bf16[8,8,112]{2,1,0:T(8,128)(2,1)S(1)}, u32[]{:S(2)}, u32[]{:S(2)}) async-start(bf16[8,8,112]{2,1,0:T(8,128)(2,1)} %bitcast.30), calls=%async_computation.7 | async-start | bytes 32768 | tf_op jit(solution)/shard_map/all_to_all | solution.py:180
  474.6 34.0 %copy-start.16 = (bf16[4,20,256]{2,0,1:T(4,128)(2,1)S(1)}, bf16[4,20,256]{2,0,1:T(4,128)(2,1)}, u32[]{:S(2)}) copy-start(bf16[4,20,256]{2,0,1:T(4,128)(2,1)} %param.32) | copy-start | bytes 122884
  475.8 33.0 %copy-start.4 = (bf16[4,256,256]{2,1,0:T(8,128)(2,1)S(1)}, bf16[4,256,256]{2,1,0:T(8,128)(2,1)}, u32[]{:S(2)}) copy-start(bf16[4,256,256]{2,1,0:T(8,128)(2,1)} %param.33) | copy-start | bytes 1572868
  475.8 7.2 %all-to-all-start.1 = ((bf16[4,2,576]{2,1,0:T(2,128)(2,1)}), bf16[4,2,576]{2,1,0:T(2,128)(2,1)S(1)}, u32[]{:S(2)}, u32[]{:S(2)}) async-start(bf16[4,2,576]{2,1,0:T(2,128)(2,1)} %reshape.298), calls=%async_computation.5 | async-start | bytes 20480 | tf_op jit(solution)/shard_map/all_to_all | solution.py:163
  483.7 25.3 %copy-start.5 = (bf16[4,256,256]{2,1,0:T(8,128)(2,1)S(1)}, bf16[4,256,256]{2,1,0:T(8,128)(2,1)}, u32[]{:S(2)}) copy-start(bf16[4,256,256]{2,1,0:T(8,128)(2,1)} %param.34) | copy-start | bytes 1572868
  485.8 12.2 %all-to-all-start.2 = ((bf16[8,8,192]{2,1,0:T(8,128)(2,1)}), bf16[8,8,192]{2,1,0:T(8,128)(2,1)S(1)}, u32[]{:S(2)}, u32[]{:S(2)}) async-start(bf16[8,8,192]{2,1,0:T(8,128)(2,1)} %reshape.234), calls=%async_computation.6 | async-start | bytes 65536 | tf_op jit(solution)/shard_map/all_to_all | solution.py:173
  516.9 10.0 %all-to-all-start.4 = ((bf16[8,8,192]{2,1,0:T(8,128)(2,1)}), bf16[8,8,192]{2,1,0:T(8,128)(2,1)S(1)}, u32[]{:S(2)}, u32[]{:S(2)}) async-start(bf16[8,8,192]{2,1,0:T(8,128)(2,1)} %copy.237), calls=%async_computation.8 | async-start | bytes 65536 | tf_op jit(solution)/shard_map/all_to_all | solution.py:252
  528.0 7.1 %all-to-all-start.5 = ((bf16[12,2,192]{2,1,0:T(2,128)(2,1)}), bf16[12,2,192]{2,1,0:T(2,128)(2,1)S(1)}, u32[]{:S(2)}, u32[]{:S(2)}) async-start(bf16[12,2,192]{2,1,0:T(2,128)(2,1)} %gather_fusion), calls=%async_computation.9 | async-start | bytes 24576 | tf_op jit(solution)/shard_map/all_to_all | solution.py:254
  (18 other events, 94.3 us)
Sparse Core Ops, SparseCore 0:
  13.4 20.1 all-gather.17
  108.5 24.7 reduce-scatter.4
  217.6 25.6 reduce-scatter.6
  335.7 24.2 reduce-scatter.8
  444.2 25.6 reduce-scatter.10
Sparse Core Ops, SparseCore 1:
  111.6 40.5 all-gather.25
  154.8 39.7 all-gather.27
  196.5 15.6 all-gather.19
  245.6 17.3 all-gather.21
  338.5 40.0 all-gather.29
  381.4 39.7 all-gather.31
  423.2 15.6 all-gather.23
where the time goes:
time: 544 us; the launch traced here: 543 us
  waiting for transfers between devices  254 us (47%)
  blocking collectives  157 us (29%)
  matrix products  37.6 us (7%)
  local copies, waits for them, and re-layouts  33.4 us (6%)
  starting transfers between devices  25.1 us (5%)
  other arithmetic  19.4 us (4%)
  between operations  15.9 us (3%)
    all_gather x2, waiting for transfers between devices, on_device(): lax.all_gather(mlp_out[layer_index], 'dp', axis=1, tiled=True)  85 us
    reduce_scatter x4, waiting for transfers between devices, reduce_rows(): lax.psum_scatter(partial_value.astype(jnp.bfloat16), 'mp', scatter_dimens...  80 us
    all_gather x2, blocking collectives, on_device(): lax.all_gather(attn_in[layer_index], 'dp', axis=1, tiled=True)  77.4 us
    all_gather x2, blocking collectives, on_device(): lax.all_gather(attn_out[layer_index], 'dp', axis=1, tiled=True)  64.3 us
    all_gather x4, waiting for transfers between devices, gather_rows(): lax.all_gather(normed, 'mp', axis=0, tiled=True)  35.4 us
    all_gather x2, waiting for transfers between devices, on_device(): lax.all_gather(mlp_in[layer_index], 'dp', axis=0, tiled=True)  30.9 us
  transfers between devices with their start and end apart: 18, of which 15 were waited for; matrix products, arithmetic and copies ran while one was open for 6% of the time, Pallas kernels for 0%

commit v1 on v0

--- a/solution.py
+++ b/solution.py
@@ -12,6 +12,22 @@
 ADIM_MAX = 14
 ACT = 56
 norm_eps = 1e-05
+
+
+def ring_product(array, axis, dim, term):
+    devices, mine, width = (lax.axis_size(axis), lax.axis_index(axis), array.shape[dim])
+    upward = [(i, (i + 1) % devices) for i in range(devices)]
+    downward = [(i, (i - 1) % devices) for i in range(devices)]
+    halfway = devices // 2
+    from_left = from_right = array
+    total = term(array, mine * width)
+    for hop in range(1, halfway + 1):
+        from_left = lax.ppermute(from_left, axis, upward)
+        if hop < devices - halfway:
+            from_right = lax.ppermute(from_right, axis, downward)
+            total = total + term(from_right, (mine + hop) % devices * width)
+        total = total + term(from_left, (mine - hop) % devices * width)
+    return total
 
 
 def normalize(values, scale_gain):
@@ -120,11 +136,16 @@
         gathered, mask_group = gather_rows(normed, obs_mask)
         samples_group = mask_group.shape[0]
         columns = gathered
-        projected = jnp.einsum(
-            "td,jdc->jtc",
-            columns,
-            lax.all_gather(attn_in[layer_index], "dp", axis=1, tiled=True),
-            preferred_element_type=jnp.float32,
+        projected = ring_product(
+            attn_in[layer_index],
+            "dp",
+            1,
+            lambda own_block, at: jnp.einsum(
+                "td,jdc->jtc",
+                lax.dynamic_slice_in_dim(columns, at, own_block.shape[1], axis=1),
+                own_block,
+                preferred_element_type=jnp.float32,
+            ),
         )
         projected = projected.astype(jnp.bfloat16).reshape(
             3, samples_group, length, heads_local, HDIM

time: 544 us -> 523 us (0.961)
  blocking collectives: 157 us -> 81.9 us
  starting transfers between devices: 25.1 us -> 56.1 us
  waiting for transfers between devices: 254 us -> 276 us
  matrix products: 37.6 us -> 45.8 us
  local copies, waits for them, and re-layouts: 33.4 us -> 27.7 us
    all_gather x2 -> x0, blocking collectives: 77.4 us -> none  [on_device(): lax.all_gather(attn_in[layer_index], 'dp', axis=1, tiled=True)]
    ppermute x0 -> x14, starting transfers between devices: none -> 30.8 us  [the longest x6 26.6 us: ring_product(): from_right = lax.ppermute(from_right, axis, downward)]
    ppermute x0 -> x14, waiting for transfers between devices: none -> 17.6 us  [the longest x8 11.2 us: ring_product(): from_left = lax.ppermute(from_left, axis, upward)]
    unnamed x2 -> x16, matrix products: 4.58 us -> 12.6 us
  transfers between devices with their start and end apart: 18 -> 32, of which waited for: 15 -> 21; matrix products, arithmetic and copies ran while one was open for 6% -> 6% of each run, Pallas kernels for 0% -> 0%
where the time goes in v1:
time: 523 us; the launch traced here: 521 us
  waiting for transfers between devices  276 us (53%)
  blocking collectives  81.9 us (16%)
  starting transfers between devices  56.1 us (11%)
  matrix products  45.8 us (9%)
  local copies, waits for them, and re-layouts  27.7 us (5%)
  other arithmetic  17.7 us (3%)
  between operations  16.1 us (3%)
    all_gather x2, waiting for transfers between devices, on_device(): lax.all_gather(mlp_out[layer_index], 'dp', axis=1, tiled=True)  85 us
    reduce_scatter x4, waiting for transfers between devices, reduce_rows(): lax.psum_scatter(partial_value.astype(jnp.bfloat16), 'mp', scatter_dimens...  84.4 us
    all_gather x2, blocking collectives, on_device(): lax.all_gather(attn_out[layer_index], 'dp', axis=1, tiled=True)  66.5 us
    all_gather x4, waiting for transfers between devices, gather_rows(): lax.all_gather(normed, 'mp', axis=0, tiled=True)  35.4 us
    all_gather x2, waiting for transfers between devices, on_device(): lax.all_gather(mlp_in[layer_index], 'dp', axis=0, tiled=True)  30.5 us
    ppermute x6, starting transfers between devices, ring_product(): from_right = lax.ppermute(from_right, axis, downward)  26.6 us
    unnamed x16, matrix products  12.6 us
    ppermute x8, waiting for transfers between devices, ring_product(): from_left = lax.ppermute(from_left, axis, upward)  11.2 us
  transfers between devices with their start and end apart: 32, of which 21 were waited for; matrix products, arithmetic and copies ran while one was open for 6% of the time, Pallas kernels for 0%

profile of v1, /device:TPU:0, one launch (start us, length us, event | category | flops | bytes accessed | tf_op | source)
XLA Modules:
  0.0 521.5 jit_solution(13579531374184712711)
XLA Ops:
  20.4 5.2 all-gather.6
  26.3 8.8 %collective-permute-done.3 = bf16[3,96,192]{1,2,0:T(8,128)(2,1)S(1)} collective-permute-done((bf16[3,96,192]{1,2,0:T(8,128)(2,1)S(1)}, bf16[3,96,192]{1,2,0:T(8,128)(2,1)S(1)}, u32[]{:S(2)}, u32[]{:S(2)}) %collective-permute-start.3) | collective-permute-done | bytes 110624 | tf_op jit(solution)/shard_map/ppermute | solution.py:25
  36.0 4.8 collective-permute-start.2
  43.8 32.7 %all-gather = bf16[1,192,768]{1,0,2:T(2,128)(2,1)S(1)} all-gather(bf16[1,192,96]{1,0,2:T(2,128)(2,1)S(1)} %copy.361), channel_id=2, replica_groups=mesh['dp'=8,'mp'=4] {'dp'}, dimensions={2}, use_global_device_ids=true | all-gather | bytes 331776 | tf_op jit(solution)/shard_map/all_gather | solution.py:158
  100.1 26.0 %reduce-scatter.13.cloned.1.call-done = bf16[192,768]{1,0:T(8,128)(2,1)} async-done(((bf16[768,768]{1,0:T(8,128)(2,1)}), bf16[192,768]{1,0:T(8,128)(2,1)}) %reduce-scatter.13.cloned.1.call-update) | async-done | bytes 294928 | tf_op jit(solution)/shard_map/reduce_scatter | solution.py:94
  129.7 15.4 %all-gather.24.cloned.1.call-done = bf16[1,768,768]{2,1,0:T(8,128)(2,1)} async-done(((bf16[1,96,768]{2,1,0:T(8,128)(2,1)}), bf16[1,768,768]{2,1,0:T(8,128)(2,1)}) %all-gather.24.cloned.1.call-update) | async-done | bytes 1179664 | tf_op jit(solution)/shard_map/all_gather | solution.py:166
  145.1 42.4 %all-gather.26.cloned.1.call-done = bf16[1,768,768]{1,2,0:T(8,128)(2,1)} async-done(((bf16[1,768,96]{1,2,0:T(8,128)(2,1)}), bf16[1,768,768]{1,2,0:T(8,128)(2,1)}) %all-gather.26.cloned.1.call-update) | async-done | bytes 1179664 | tf_op jit(solution)/shard_map/all_gather | solution.py:172
  187.5 17.7 %all-gather.18.cloned.1.call-done = bf16[768,768]{1,0:T(8,128)(2,1)} async-done(((bf16[192,768]{1,0:T(8,128)(2,1)}), bf16[768,768]{1,0:T(8,128)(2,1)}) %all-gather.18.cloned.1.call-update) | async-done | bytes 1179664 | tf_op jit(solution)/shard_map/all_gather | solution.py:88
  205.2 5.2 convolution_convert_fusion.2
  210.5 25.7 %reduce-scatter.15.cloned.1.call-done = bf16[192,768]{1,0:T(8,128)(2,1)} async-done(((bf16[768,768]{1,0:T(8,128)(2,1)}), bf16[192,768]{1,0:T(8,128)(2,1)}) %reduce-scatter.15.cloned.1.call-update) | async-done | bytes 294928 | tf_op jit(solution)/shard_map/reduce_scatter | solution.py:94
  246.0 5.3 %collective-permute-start.9 = (bf16[3,96,192]{1,2,0:T(8,128)(2,1)S(1)}, bf16[3,96,192]{1,2,0:T(8,128)(2,1)}, u32[]{:S(2)}, u32[]{:S(2)}) collective-permute-start(bf16[3,96,192]{1,2,0:T(8,128)(2,1)S(1)} %collective-permute-done.7), channel_id=1, source_target_pairs={{0,28},{4,0},{8,4},{12,8},{16,12},{20,16},{24,20},{28,24},{1,29},{... | collective-permute-start | bytes 331784 | tf_op jit(solution)/shard_map/ppermute | solution.py:27
  253.9 5.4 %collective-permute-start.11 = (bf16[3,96,192]{1,2,0:T(8,128)(2,1)}, bf16[3,96,192]{1,2,0:T(8,128)(2,1)}, u32[]{:S(2)}, u32[]{:S(2)}) collective-permute-start(bf16[3,96,192]{1,2,0:T(8,128)(2,1)} %collective-permute-done.9), channel_id=1, source_target_pairs={{0,28},{4,0},{8,4},{12,8},{16,12},{20,16},{24,20},{28,24},{1,29},{... | collective-permute-start | bytes 331784 | tf_op jit(solution)/shard_map/ppermute | solution.py:27
  259.3 33.8 %all-gather.3 = bf16[1,192,768]{1,0,2:T(2,128)(2,1)S(1)} all-gather(bf16[1,192,96]{1,0,2:T(2,128)(2,1)S(1)} %copy.371), channel_id=5, replica_groups=mesh['dp'=8,'mp'=4] {'dp'}, dimensions={2}, use_global_device_ids=true | all-gather | bytes 331776 | tf_op jit(solution)/shard_map/all_gather | solution.py:158
  317.2 24.4 %reduce-scatter.17.cloned.1.call-done = bf16[192,768]{1,0:T(8,128)(2,1)} async-done(((bf16[768,768]{1,0:T(8,128)(2,1)}), bf16[192,768]{1,0:T(8,128)(2,1)}) %reduce-scatter.17.cloned.1.call-update) | async-done | bytes 294928 | tf_op jit(solution)/shard_map/reduce_scatter | solution.py:94
  345.1 15.1 %all-gather.28.cloned.1.call-done = bf16[1,768,768]{2,1,0:T(8,128)(2,1)} async-done(((bf16[1,96,768]{2,1,0:T(8,128)(2,1)}), bf16[1,768,768]{2,1,0:T(8,128)(2,1)}) %all-gather.28.cloned.1.call-update) | async-done | bytes 1179664 | tf_op jit(solution)/shard_map/all_gather | solution.py:166
  360.1 42.6 %all-gather.30.cloned.1.call-done = bf16[1,768,768]{1,2,0:T(8,128)(2,1)} async-done(((bf16[1,768,96]{1,2,0:T(8,128)(2,1)}), bf16[1,768,768]{1,2,0:T(8,128)(2,1)}) %all-gather.30.cloned.1.call-update) | async-done | bytes 1179664 | tf_op jit(solution)/shard_map/all_gather | solution.py:172
  402.7 17.7 %all-gather.22.cloned.1.call-done = bf16[768,768]{1,0:T(8,128)(2,1)} async-done(((bf16[192,768]{1,0:T(8,128)(2,1)}), bf16[768,768]{1,0:T(8,128)(2,1)}) %all-gather.22.cloned.1.call-update) | async-done | bytes 1179664 | tf_op jit(solution)/shard_map/all_gather | solution.py:88
  420.4 5.2 convolution_convert_fusion
  427.7 5.5 %all-to-all-start = ((s32[8,1,8]{2,1,0:T(1,128)}), s32[8,1,8]{2,1,0:T(1,128)S(1)}, u32[]{:S(2)}, u32[]{:S(2)}) async-start(s32[8,1,8]{2,1,0:T(1,128)} %bitcast.1), calls=%async_computation | async-start | bytes 8192 | tf_op jit(solution)/shard_map/all_to_all | solution.py:208
  443.1 8.3 %reduce-scatter.19.cloned.1.call-done = bf16[192,768]{1,0:T(8,128)(2,1)} async-done(((bf16[768,768]{1,0:T(8,128)(2,1)}), bf16[192,768]{1,0:T(8,128)(2,1)}) %reduce-scatter.19.cloned.1.call-update) | async-done | bytes 294928 | tf_op jit(solution)/shard_map/reduce_scatter | solution.py:94
  464.3 5.5 %all-to-all-start.2 = ((bf16[8,8,192]{2,1,0:T(8,128)(2,1)}), bf16[8,8,192]{2,1,0:T(8,128)(2,1)S(1)}, u32[]{:S(2)}, u32[]{:S(2)}) async-start(bf16[8,8,192]{2,1,0:T(8,128)(2,1)} %reshape.234), calls=%async_computation.2 | async-start | bytes 65536 | tf_op jit(solution)/shard_map/all_to_all | solution.py:194
  470.0 6.5 %all-to-all-done.2 = bf16[8,8,192]{2,1,0:T(8,128)(2,1)S(1)} async-done(((bf16[8,8,192]{2,1,0:T(8,128)(2,1)}), bf16[8,8,192]{2,1,0:T(8,128)(2,1)S(1)}, u32[]{:S(2)}, u32[]{:S(2)}) %all-to-all-start.2) | async-done | bytes 24608 | tf_op jit(solution)/shard_map/all_to_all | solution.py:194
  476.8 10.3 %psum.7 = bf16[4,16,256]{2,1,0:T(8,128)(2,1)S(1)} all-reduce(bf16[4,16,256]{2,1,0:T(8,128)(2,1)S(1)} %convolution_convert_fusion.10), channel_id=1, replica_groups=mesh['dp'=8,'mp'=4] {'mp'}, use_global_device_ids=true, to_apply=%region_19.20 | all-reduce | flops 16384 | bytes 65536 | tf_op jit(solution)/shard_map/psum | solution.py:243
  499.7 5.7 %all-to-all-done.4 = bf16[8,8,192]{2,1,0:T(8,128)(2,1)S(1)} async-done(((bf16[8,8,192]{2,1,0:T(8,128)(2,1)}), bf16[8,8,192]{2,1,0:T(8,128)(2,1)S(1)}, u32[]{:S(2)}, u32[]{:S(2)}) %all-to-all-start.4) | async-done | bytes 24608 | tf_op jit(solution)/shard_map/all_to_all | solution.py:273
  (246 shorter events, 130.2 us)
Async XLA Ops:
  8.0 72.8 %all-gather.16.cloned.1.call-start = ((), (), s32[]{:S(2)}) async-start(), calls=%async_computation.10 | async-start | bytes 1474560 | tf_op jit(solution)/shard_map/all_gather | solution.py:88
  13.3 112.9 %reduce-scatter.13.cloned.1.call-start = ((), (), s32[]{:S(2)}) async-start(), calls=%async_computation.18 | async-start | bytes 1474560 | tf_op jit(solution)/shard_map/reduce_scatter | solution.py:94
  14.2 12.0 %collective-permute-start.1 = (bf16[3,96,192]{1,2,0:T(8,128)(2,1)S(1)}, bf16[3,96,192]{1,2,0:T(8,128)(2,1)S(1)}, u32[]{:S(2)}, u32[]{:S(2)}) collective-permute-start(bf16[3,96,192]{1,2,0:T(8,128)(2,1)S(1)} %bitcast.213), channel_id=1, source_target_pairs={{0,4},{4,8},{8,12},{12,16},{16,20},{20,24},{24,28},{28,0},{1,5},{5... | collective-permute-start | bytes 331784 | tf_op jit(solution)/shard_map/ppermute | solution.py:25
  17.3 18.7 %collective-permute-start = (bf16[3,96,192]{1,2,0:T(8,128)(2,1)S(1)}, bf16[3,96,192]{1,2,0:T(8,128)(2,1)S(1)}, u32[]{:S(2)}, u32[]{:S(2)}) collective-permute-start(bf16[3,96,192]{1,2,0:T(8,128)(2,1)S(1)} %bitcast.214), channel_id=1, source_target_pairs={{0,28},{4,0},{8,4},{12,8},{16,12},{20,16},{24,20},{28,24},{1,29},{... | collective-permute-start | bytes 331784 | tf_op jit(solution)/shard_map/ppermute | solution.py:27
  26.2 8.8 %collective-permute-start.3 = (bf16[3,96,192]{1,2,0:T(8,128)(2,1)S(1)}, bf16[3,96,192]{1,2,0:T(8,128)(2,1)S(1)}, u32[]{:S(2)}, u32[]{:S(2)}) collective-permute-start(bf16[3,96,192]{1,2,0:T(8,128)(2,1)S(1)} %collective-permute-done.1), channel_id=1, source_target_pairs={{0,4},{4,8},{8,12},{12,16},{16,20},{20,24},{24,28},{28,0},{1,5},{5... | collective-permute-start | bytes 331784 | tf_op jit(solution)/shard_map/ppermute | solution.py:25
  36.0 40.9 %collective-permute-start.2 = (bf16[3,96,192]{1,2,0:T(8,128)(2,1)S(1)}, bf16[3,96,192]{1,2,0:T(8,128)(2,1)S(1)}, u32[]{:S(2)}, u32[]{:S(2)}) collective-permute-start(bf16[3,96,192]{1,2,0:T(8,128)(2,1)S(1)} %collective-permute-done), channel_id=1, source_target_pairs={{0,28},{4,0},{8,4},{12,8},{16,12},{20,16},{24,20},{28,24},{1,29},{... | collective-permute-start | bytes 331784 | tf_op jit(solution)/shard_map/ppermute | solution.py:27
  43.1 37.7 %collective-permute-start.6 = (bf16[3,96,192]{1,2,0:T(8,128)(2,1)S(1)}, bf16[3,96,192]{1,2,0:T(8,128)(2,1)}, u32[]{:S(2)}, u32[]{:S(2)}) collective-permute-start(bf16[3,96,192]{1,2,0:T(8,128)(2,1)S(1)} %collective-permute-done.5), channel_id=1, source_target_pairs={{0,4},{4,8},{8,12},{12,16},{16,20},{20,24},{24,28},{28,0},{1,5},{5... | collective-permute-start | bytes 331784 | tf_op jit(solution)/shard_map/ppermute | solution.py:25
  98.4 46.7 %all-gather.24.cloned.1.call-start = ((), (), s32[]{:S(2)}) async-start(), calls=%async_computation.14 | async-start | bytes 1327104 | tf_op jit(solution)/shard_map/all_gather | solution.py:166
  99.2 88.3 %all-gather.26.cloned.1.call-start = ((), (), s32[]{:S(2)}) async-start(), calls=%async_computation.15 | async-start | bytes 1327104 | tf_op jit(solution)/shard_map/all_gather | solution.py:172
  100.1 105.1 %all-gather.18.cloned.1.call-start = ((), (), s32[]{:S(2)}) async-start(), calls=%async_computation.11 | async-start | bytes 1474560 | tf_op jit(solution)/shard_map/all_gather | solution.py:88
  129.5 106.8 %reduce-scatter.15.cloned.1.call-start = ((), (), s32[]{:S(2)}) async-start(), calls=%async_computation.19 | async-start | bytes 1474560 | tf_op jit(solution)/shard_map/reduce_scatter | solution.py:94
  210.5 83.5 %all-gather.20.cloned.1.call-start = ((), (), s32[]{:S(2)}) async-start(), calls=%async_computation.12 | async-start | bytes 1474560 | tf_op jit(solution)/shard_map/all_gather | solution.py:88
  238.5 103.0 %reduce-scatter.17.cloned.1.call-start = ((), (), s32[]{:S(2)}) async-start(), calls=%async_computation.20 | async-start | bytes 1474560 | tf_op jit(solution)/shard_map/reduce_scatter | solution.py:94
  243.0 8.2 %collective-permute-start.8 = (bf16[3,96,192]{1,2,0:T(8,128)(2,1)S(1)}, bf16[3,96,192]{1,2,0:T(8,128)(2,1)S(1)}, u32[]{:S(2)}, u32[]{:S(2)}) collective-permute-start(bf16[3,96,192]{1,2,0:T(8,128)(2,1)S(1)} %bitcast.217), channel_id=1, source_target_pairs={{0,4},{4,8},{8,12},{12,16},{16,20},{20,24},{24,28},{28,0},{1,5},{5... | collective-permute-start | bytes 331784 | tf_op jit(solution)/shard_map/ppermute | solution.py:25
  253.9 40.0 %collective-permute-start.11 = (bf16[3,96,192]{1,2,0:T(8,128)(2,1)}, bf16[3,96,192]{1,2,0:T(8,128)(2,1)}, u32[]{:S(2)}, u32[]{:S(2)}) collective-permute-start(bf16[3,96,192]{1,2,0:T(8,128)(2,1)} %collective-permute-done.9), channel_id=1, source_target_pairs={{0,28},{4,0},{8,4},{12,8},{16,12},{20,16},{24,20},{28,24},{1,29},{... | collective-permute-start | bytes 331784 | tf_op jit(solution)/shard_map/ppermute | solution.py:27
  259.3 34.3 %collective-permute-start.12 = (bf16[3,96,192]{1,2,0:T(8,128)(2,1)}, bf16[3,96,192]{1,2,0:T(8,128)(2,1)}, u32[]{:S(2)}, u32[]{:S(2)}) collective-permute-start(bf16[3,96,192]{1,2,0:T(8,128)(2,1)} %collective-permute-done.10), channel_id=1, source_target_pairs={{0,4},{4,8},{8,12},{12,16},{16,20},{20,24},{24,28},{28,0},{1,5},{5... | collective-permute-start | bytes 331784 | tf_op jit(solution)/shard_map/ppermute | solution.py:25
  315.6 44.5 %all-gather.28.cloned.1.call-start = ((), (), s32[]{:S(2)}) async-start(), calls=%async_computation.16 | async-start | bytes 1327104 | tf_op jit(solution)/shard_map/all_gather | solution.py:166
  316.4 86.3 %all-gather.30.cloned.1.call-start = ((), (), s32[]{:S(2)}) async-start(), calls=%async_computation.17 | async-start | bytes 1327104 | tf_op jit(solution)/shard_map/all_gather | solution.py:172
  317.1 103.3 %all-gather.22.cloned.1.call-start = ((), (), s32[]{:S(2)}) async-start(), calls=%async_computation.13 | async-start | bytes 1474560 | tf_op jit(solution)/shard_map/all_gather | solution.py:88
  344.8 106.6 %reduce-scatter.19.cloned.1.call-start = ((), (), s32[]{:S(2)}) async-start(), calls=%async_computation.21 | async-start | bytes 1474560 | tf_op jit(solution)/shard_map/reduce_scatter | solution.py:94
  427.7 11.9 %all-to-all-start = ((s32[8,1,8]{2,1,0:T(1,128)}), s32[8,1,8]{2,1,0:T(1,128)S(1)}, u32[]{:S(2)}, u32[]{:S(2)}) async-start(s32[8,1,8]{2,1,0:T(1,128)} %bitcast.1), calls=%async_computation | async-start | bytes 8192 | tf_op jit(solution)/shard_map/all_to_all | solution.py:208
  439.6 14.8 %all-to-all-start.3 = ((bf16[8,8,112]{2,1,0:T(8,128)(2,1)}), bf16[8,8,112]{2,1,0:T(8,128)(2,1)S(1)}, u32[]{:S(2)}, u32[]{:S(2)}) async-start(bf16[8,8,112]{2,1,0:T(8,128)(2,1)} %bitcast.72), calls=%async_computation.3 | async-start | bytes 32768 | tf_op jit(solution)/shard_map/all_to_all | solution.py:201
  464.3 12.2 %all-to-all-start.2 = ((bf16[8,8,192]{2,1,0:T(8,128)(2,1)}), bf16[8,8,192]{2,1,0:T(8,128)(2,1)S(1)}, u32[]{:S(2)}, u32[]{:S(2)}) async-start(bf16[8,8,192]{2,1,0:T(8,128)(2,1)} %reshape.234), calls=%async_computation.2 | async-start | bytes 65536 | tf_op jit(solution)/shard_map/all_to_all | solution.py:194
  495.4 10.0 %all-to-all-start.4 = ((bf16[8,8,192]{2,1,0:T(8,128)(2,1)}), bf16[8,8,192]{2,1,0:T(8,128)(2,1)S(1)}, u32[]{:S(2)}, u32[]{:S(2)}) async-start(bf16[8,8,192]{2,1,0:T(8,128)(2,1)} %copy.339), calls=%async_computation.4 | async-start | bytes 65536 | tf_op jit(solution)/shard_map/all_to_all | solution.py:273
  (34 other events, 780.5 us)
Sparse Core Ops, SparseCore 0:
  13.4 20.1 all-gather.15
  98.5 27.6 reduce-scatter.12
  210.6 25.6 reduce-scatter.14
  315.7 25.7 reduce-scatter.16
  425.8 25.6 reduce-scatter.18
Sparse Core Ops, SparseCore 1:
  101.6 43.4 all-gather.23
  147.7 39.7 all-gather.25
  189.5 15.6 all-gather.17
  238.6 17.3 all-gather.19
  318.6 41.5 all-gather.27
  362.9 39.7 all-gather.29
  404.7 15.6 all-gather.21
